TPU v7x, 128 devices: a whole 4x4x4 slice. The times are simulated.
128 devices in a mesh: group: 4 (over z), sub: 32 (over y, x, core).
Axes of the slice: x: 4, y: 4, z: 4, core: 2. Of those that a mesh axis runs over, the one named last changes fastest.
Arguments:
- displacement: float32 [3, 35, 131072], P(None, None, ('group', 'sub')), may hold values from -6 to 6
- velocity: float32 [3, 35, 131072], P(None, None, ('group', 'sub')), may hold values from -6 to 6
- geometry_weights: float32 [6, 131072], P(None, ('group', 'sub')), may hold values from 0.2 to 2
- jacobian: float32 [131072], P(('group', 'sub')), may hold values from 0.5 to 2
- strain_map: float32 [630, 105], replicated, may hold values from -0.25 to 0.25
- face_mass: float32 [15, 15], replicated, may hold values from -1 to 2, as said below
- mass_inverse: float32 [35, 35], replicated, may hold values from -1 to 2, as said below
- local_links: int32 [2, 393216], P(None, ('group', 'sub')), may hold values from 0 to 383, as said below
- local_geometry: float32 [4, 393216], P(None, ('group', 'sub')), may hold values from -1 to 3, as said below
- neighbour_links: int32 [2, 16384], P(None, ('group', 'sub')), may hold values from 0 to 2, as said below
- neighbour_geometry: float32 [8, 16384], P(None, ('group', 'sub')), may hold values from -1 to 3, as said below
- cross_links: int32 [98304], P(('group', 'sub')), may hold values from 0 to 2, as said below
- cross_geometry: float32 [4, 98304], P(None, ('group', 'sub')), may hold values from -1 to 3, as said below
Outputs:
- displacement_new: float32 [3, 35, 131072], P(None, None, ('group', 'sub'))
- velocity_new: float32 [3, 35, 131072], P(None, None, ('group', 'sub'))
Inputs may be any that keep to these rules, and one draw needn't show every extreme that they name: `local_links`: row 0 is the partner inside the same aligned block of 128 elements, as the steps read it; the pairing is symmetric and never pairs a half-face with itself. Row 1 is the state (0 intact, 1 cohesive, 2 broken), equal on both half-faces of a pair. `local_geometry`: rows 0 to 2 are a unit normal, row 3 a positive scale; both half-faces of a pair hold the same values. `neighbour_links`: row 0: state of the upper shared half-face, row 1: of the lower one (0 intact, 1 cohesive, 2 broken). Row 1 of device (g, s) equals row 0 of the same column on device (g, (s - 1) mod 32). `neighbour_geometry`: rows 0 to 3: unit normal and positive scale of the upper half-face; rows 4 to 7 of device (g, s) equal rows 0 to 3 of the same column on device (g, (s - 1) mod 32). `cross_links`: states (0 intact, 1 cohesive, 2 broken). In the block of 8 slots that a device holds for one partner device, the first count slots hold faces and the rest are padding with state 2; count is the same on both sides of a pair, 1 to 8, 8 for some pair, and the states of matching slots agree. `cross_geometry`: rows 0 to 2 a unit normal, row 3 a positive scale; matching slots of a pair hold the same values. `face_mass`: Symmetric. `mass_inverse`: Symmetric.
All inputs are finite; a program needn't handle non-finite values.
Results may differ from a plain program's by a relative error of at most 0.00011.
Values sent between devices are 32-bit elements; how exact they have to be, the bound alone decides.
A program may use at most 128 MiB of HBM per device.

v0:
```python
import jax
import jax.numpy as jnp
import numpy as np
from jax import lax
from jax.sharding import PartitionSpec as P

BLOCK = 128
STEPS = 5


shear_weight = 0.5
opening_scale = 4.0
time_step = 0.25
highest = lax.Precision.HIGHEST


def shifted(value, axis, steps):
    count = lax.axis_size(axis)
    pairs = [(source, (source + steps) % count) for source in range(count)]
    return lax.ppermute(value, axis, pairs)


def face_table():
    points = [
        (first, second, third, 4 - first - second - third)
        for first in range(5)
        for second in range(5 - first)
        for third in range(5 - first - second)
    ]
    result = np.zeros((4, 15, 35), np.float32)
    for side in range(4):
        members = [index for index, point in enumerate(points) if point[side] == 0]
        for place, index in enumerate(members):
            result[side, place, index] = 1.0
    return result


def cohesive_traction(jump, normal, state):
    along = jnp.sum(normal[:, None, :] * jump, axis=0)
    normal_part = along[None] * normal[:, None, :]
    tangent = jump - normal_part
    opening = along * along + shear_weight * jnp.sum(tangent * tangent, axis=0)
    softened = jnp.exp(-opening / opening_scale)[None] * (normal_part + shear_weight * tangent)
    zeros = jnp.zeros_like(jump)
    return jnp.where(
        state[None, None, :] == 0, jump, jnp.where(state[None, None, :] == 1, softened, zeros)
    )


def apply_mass(traction, scale, face_mass):
    spread = jnp.einsum("ij,cjf->cif", face_mass, traction, precision=highest)
    return scale[None, None, :] * spread


def face_force(jump, geometry, state, face_mass):
    return apply_mass(cohesive_traction(jump, geometry[0:3], state), geometry[3], face_mass)


def shards(
    displacement,
    velocity,
    geometry_weights,
    jacobian,
    strain_map,
    face_mass,
    mass_inverse,
    local_links,
    local_geometry,
    neighbour_links,
    neighbour_geometry,
    cross_links,
    cross_geometry,
):
    table = jnp.asarray(face_table())
    components = displacement.shape[0]
    node_count = displacement.shape[1]
    elements = displacement.shape[2]
    face_nodes = table.shape[1]
    pieces = strain_map.shape[0] // (components * node_count)
    groups = lax.axis_size("group")
    slots = cross_links.shape[0]
    shared = neighbour_links.shape[1]
    width = slots // (groups - 1)
    spare = elements - 2 * shared - slots
    count_blocks = elements // BLOCK
    own_group = lax.axis_index("group")
    partner = jnp.transpose(local_links[0].reshape(3, count_blocks, BLOCK), (1, 0, 2))
    labels = (
        jnp.arange(3, dtype=jnp.int32)[:, None] * BLOCK
        + jnp.arange(BLOCK, dtype=jnp.int32)[None, :]
    )
    selector = (partner[:, None, None, :, :] == labels[None, :, :, None, None]).astype(jnp.float32)
    filler = jnp.zeros((components, face_nodes, spare), jnp.float32)
    field = displacement
    for step in range(STEPS):
        traces = jnp.einsum("kin,cne->cike", table, field, precision=highest)
        own_local = traces[:, :, 1:]
        paired = jnp.einsum(
            "cikjb,jkbql->ciqjl",
            own_local.reshape(components, face_nodes, 3, count_blocks, BLOCK),
            selector,
            precision=highest,
        )
        jump = paired.reshape(components, face_nodes, 3 * elements) - own_local.reshape(
            components, face_nodes, 3 * elements
        )
        local_force = face_force(jump, local_geometry, local_links[1], face_mass)
        rim = traces[:, :, 0]
        upper = rim[:, :, 0:shared]
        lower = rim[:, :, shared : 2 * shared]
        outgoing = rim[:, :, 2 * shared : 2 * shared + slots]
        arrived = shifted(lower, "sub", -1)
        upper_force = face_force(
            arrived - upper, neighbour_geometry[0:4], neighbour_links[0], face_mass
        )
        lower_force = -shifted(upper_force, "sub", 1)
        blocks = outgoing.reshape(components, face_nodes, groups - 1, width)
        padded = jnp.concatenate([blocks, jnp.zeros_like(blocks[:, :, :1])], axis=2)
        placed = jnp.roll(padded, own_group + 1, axis=2).reshape(
            components, face_nodes, groups * width
        )
        received = lax.all_to_all(placed, ("group", "sub"), split_axis=2, concat_axis=2, tiled=True)
        restored = jnp.roll(
            received.reshape(components, face_nodes, groups, width), -(own_group + 1), axis=2
        )
        incoming = restored[:, :, : groups - 1].reshape(components, face_nodes, slots)
        cross_force = face_force(incoming - outgoing, cross_geometry, cross_links, face_mass)
        rim_force = jnp.concatenate([upper_force, lower_force, cross_force, filler], axis=2)
        forces = jnp.concatenate(
            [rim_force[:, :, None], local_force.reshape(components, face_nodes, 3, elements)],
            axis=2,
        )
        face_load = jnp.einsum("kin,cike->cne", table, forces, precision=highest)
        strain = jnp.dot(
            strain_map, field.reshape(components * node_count, elements), precision=highest
        )
        weighted = (
            strain.reshape(pieces, components * node_count, elements) * geometry_weights[:, None, :]
        ).reshape(pieces * components * node_count, elements)
        volume = -jnp.dot(strain_map.T, weighted, precision=highest).reshape(
            components, node_count, elements
        )
        acceleration = (
            jnp.einsum("nm,cme->cne", mass_inverse, volume + face_load, precision=highest)
            / jacobian[None, None, :]
        )
        velocity = velocity + time_step * acceleration
        field = field + time_step * velocity
    return (field, velocity)


def solution(mesh):
    return jax.shard_map(
        shards,
        mesh=mesh,
        in_specs=(
            P(None, None, ("group", "sub")),
            P(None, None, ("group", "sub")),
            P(None, ("group", "sub")),
            P(("group", "sub")),
            P(),
            P(),
            P(),
            P(None, ("group", "sub")),
            P(None, ("group", "sub")),
            P(None, ("group", "sub")),
            P(None, ("group", "sub")),
            P(("group", "sub")),
            P(None, ("group", "sub")),
        ),
        out_specs=(P(None, None, ("group", "sub")), P(None, None, ("group", "sub"))),
        check_vma=False,
    )
```

profile of v0, /device:TPU:1, one launch (start us, length us, event | category | flops | bytes accessed | tf_op | source)
XLA Modules:
  0.0 353.6 jit_solution(15451874768887423118)
XLA Ops:
  4.5 2.9 reshape.568
  7.3 11.9 %all-to-all-start = ((f32[128,1,360]{2,1,0:T(1,128)}), f32[128,1,360]{2,1,0:T(1,128)}, u32[]{:S(2)}, u32[]{:S(2)}) async-start(f32[128,1,360]{2,1,0:T(1,128)} %reshape.568), calls=%async_computation | async-start | bytes 393216 | tf_op jit(solution)/shard_map/all_to_all | solution.py:122
  27.8 3.8 %convolution_multiply_fusion.5 = f32[6,105,1024]{2,1,0:T(8,128)} fusion(f32[6,105,105]{2,1,0:T(8,128)S(1)} %dot_general.145, f32[105,1024,1]{1,0,2:T(8,128)S(1)} %reshape.539, f32[6,1024]{1,0:T(8,128)S(1)} %copy-done.59), kind=kOutput, calls=%fused_computation.43 | convolution fusion | flops 813496320 | bytes 3299736 | tf_op jit(solution)/shard_map/dot_general | solution.py:134
  33.7 2.6 fusion.72
  52.3 3.3 reshape.569
  70.3 3.7 %fusion.368 = f32[1024,630]{0,1:T(8,128)} fusion(f32[105,1024]{1,0:T(8,128)S(1)} %copy-done.31, f32[630,105]{0,1:T(8,128)S(1)} %copy-done.1), kind=kOutput, calls=%fused_computation.526 | convolution fusion | flops 812851200 | bytes 3275160 | tf_op jit(solution)/shard_map/dot_general | solution.py:134
  76.0 3.0 multiply_reduce_fusion.7
  86.1 3.8 %reshape.570 = f32[128,1,360]{2,1,0:T(1,128)} reshape(f32[1024,3,15]{2,1,0:T(4,128)} %bitcast.441) | data formatting | bytes 368640
  89.9 12.7 %all-to-all-start.1 = ((f32[128,1,360]{2,1,0:T(1,128)}), f32[128,1,360]{2,1,0:T(1,128)}, u32[]{:S(2)}, u32[]{:S(2)}) async-start(f32[128,1,360]{2,1,0:T(1,128)} %reshape.570), calls=%async_computation.1 | async-start | bytes 393216 | tf_op jit(solution)/shard_map/all_to_all | solution.py:122
  104.5 4.7 %fusion.65 = f32[105,1024]{1,0:T(8,128)} fusion(f32[630,105]{0,1:T(8,128)S(1)} %copy-done.1, f32[630,1024]{1,0:T(8,128)S(1)} %mul.1026, f32[1024,630]{0,1:T(8,128)} %fusion.368), kind=kOutput, calls=%fused_computation.80 | convolution fusion | flops 813603840 | bytes 5855640 | tf_op jit(solution)/shard_map/dot_general | solution.py:140
  116.9 3.0 fusion.16
  129.0 3.4 reshape.571
  147.8 2.8 fusion.67
  152.5 3.0 multiply_reduce_fusion.5
  160.1 3.5 %collective-permute-start.4 = (f32[3,15,128]{2,1,0:T(8,128)}, f32[3,15,128]{2,1,0:T(8,128)S(1)}, u32[]{:S(2)}, u32[]{:S(2)}) collective-permute-start(f32[3,15,128]{2,1,0:T(8,128)} %slice.206), channel_id=1, source_target_pairs={{0,31},{1,0},{2,1},{3,2},{4,3},{5,4},{6,5},{7,6},{8,7},{9,8},{10,9... | collective-permute-start | bytes 69128 | tf_op jit(solution)/shard_map/ppermute | solution.py:20
  173.8 3.0 copy.278
  176.9 3.8 %reshape.572 = f32[128,1,360]{2,1,0:T(1,128)} reshape(f32[1024,3,15]{2,1,0:T(4,128)} %bitcast.443) | data formatting | bytes 368640
  180.7 9.8 %all-to-all-start.2 = ((f32[128,1,360]{2,1,0:T(1,128)}), f32[128,1,360]{2,1,0:T(1,128)}, u32[]{:S(2)}, u32[]{:S(2)}) async-start(f32[128,1,360]{2,1,0:T(1,128)} %reshape.572), calls=%async_computation.2 | async-start | bytes 393216 | tf_op jit(solution)/shard_map/all_to_all | solution.py:122
  194.7 3.1 fusion.17
  204.8 2.7 reduce.18
  207.5 4.1 %reshape.573 = f32[1024,3,15]{2,1,0:T(4,128)} reshape(f32[128,360]{1,0:T(8,128)} %reduce.18) | data formatting | bytes 368640
  232.0 2.8 fusion.69
  235.7 3.0 multiply_reduce_fusion.3
  253.7 2.8 copy.281
  256.5 3.8 %reshape.574 = f32[128,1,360]{2,1,0:T(1,128)} reshape(f32[1024,3,15]{2,1,0:T(4,128)} %bitcast.445) | data formatting | bytes 368640
  260.3 10.3 %all-to-all-start.3 = ((f32[128,1,360]{2,1,0:T(1,128)}), f32[128,1,360]{2,1,0:T(1,128)}, u32[]{:S(2)}, u32[]{:S(2)}) async-start(f32[128,1,360]{2,1,0:T(1,128)} %reshape.574), calls=%async_computation.3 | async-start | bytes 393216 | tf_op jit(solution)/shard_map/all_to_all | solution.py:122
  274.8 3.0 fusion.18
  286.9 3.3 reshape.575
  306.3 2.8 fusion.71
  318.5 2.9 reshape.576
  321.4 9.9 %all-to-all-start.4 = ((f32[128,1,360]{2,1,0:T(1,128)}), f32[128,1,360]{2,1,0:T(1,128)S(1)}, u32[]{:S(2)}, u32[]{:S(2)}) async-start(f32[128,1,360]{2,1,0:T(1,128)} %reshape.576), calls=%async_computation.4 | async-start | bytes 393216 | tf_op jit(solution)/shard_map/all_to_all | solution.py:122
  338.5 3.4 all-to-all-done.4
  (472 shorter events, 208.0 us)
Async XLA Ops:
  0.6 62.5 %copy-start = (f32[35,35]{1,0:T(8,128)S(1)}, f32[35,35]{1,0:T(8,128)}, u32[]{:S(2)}) copy-start(f32[35,35]{1,0:T(8,128)} %param.22) | copy-start | bytes 14704
  7.3 42.4 %all-to-all-start = ((f32[128,1,360]{2,1,0:T(1,128)}), f32[128,1,360]{2,1,0:T(1,128)}, u32[]{:S(2)}, u32[]{:S(2)}) async-start(f32[128,1,360]{2,1,0:T(1,128)} %reshape.568), calls=%async_computation | async-start | bytes 393216 | tf_op jit(solution)/shard_map/all_to_all | solution.py:122
  19.8 21.2 %collective-permute-start = (f32[3,15,128]{2,1,0:T(8,128)}, f32[3,15,128]{2,1,0:T(8,128)S(1)}, u32[]{:S(2)}, u32[]{:S(2)}) collective-permute-start(f32[3,15,128]{2,1,0:T(8,128)} %slice.196), channel_id=1, source_target_pairs={{0,31},{1,0},{2,1},{3,2},{4,3},{5,4},{6,5},{7,6},{8,7},{9,8},{10,9... | collective-permute-start | bytes 69128 | tf_op jit(solution)/shard_map/ppermute | solution.py:20
  23.6 93.2 %copy-start.38 = (f32[3,3072]{1,0:T(4,128)}, f32[3,3072]{1,0:T(4,128)S(1)}, u32[]{:S(2)}) copy-start(f32[3,3072]{1,0:T(4,128)S(1)} %get-tuple-element.6) | copy-start | bytes 110596
  23.7 128.9 %copy-start.34 = (f32[3,3,8,128]{3,0,1,2:T(4,128)}, f32[3,3,8,128]{3,0,1,2:T(4,128)S(1)}, u32[]{:S(2)}) copy-start(f32[3,3,8,128]{3,0,1,2:T(4,128)S(1)} %copy.197) | copy-start | bytes 110596
  27.5 89.4 %copy-start.54 = (f32[1,3072]{1,0:T(1,128)}, f32[1,3072]{1,0:T(1,128)S(1)}, u32[]{:S(2)}) copy-start(f32[1,3072]{1,0:T(1,128)S(1)} %slice.166) | copy-start | bytes 36868
  41.0 75.0 %copy-start.50 = (f32[3,128]{1,0:T(4,128)}, f32[3,128]{1,0:T(4,128)S(1)}, u32[]{:S(2)}) copy-start(f32[3,128]{1,0:T(4,128)S(1)} %slice.161) | copy-start | bytes 4612
  41.3 7.9 %collective-permute-start.1 = (f32[3,15,128]{2,1,0:T(8,128)S(1)}, f32[3,15,128]{2,1,0:T(8,128)S(1)}, u32[]{:S(2)}, u32[]{:S(2)}) collective-permute-start(f32[3,15,128]{2,1,0:T(8,128)S(1)} %fusion.87), channel_id=1, source_target_pairs={{0,1},{1,2},{2,3},{3,4},{4,5},{5,6},{6,7},{7,8},{8,9},{9,10},{10,1... | collective-permute-start | bytes 69128 | tf_op jit(solution)/shard_map/ppermute | solution.py:20
  82.6 20.0 %copy-start.83 = (f32[3,15,128]{2,1,0:T(8,128)S(1)}, f32[3,15,128]{2,1,0:T(8,128)}, u32[]{:S(2)}) copy-start(f32[3,15,128]{2,1,0:T(8,128)} %slice.201) | copy-start | bytes 69124
  82.6 21.2 %copy-start.47 = (f32[2,8,24,128]{3,1,2,0:T(8,128)S(1)}, f32[2,8,24,128]{3,1,2,0:T(8,128)}, u32[]{:S(2)}) copy-start(f32[2,8,24,128]{3,1,2,0:T(8,128)} %copy.291) | copy-start | bytes 589828
  89.9 37.1 %all-to-all-start.1 = ((f32[128,1,360]{2,1,0:T(1,128)}), f32[128,1,360]{2,1,0:T(1,128)}, u32[]{:S(2)}, u32[]{:S(2)}) async-start(f32[128,1,360]{2,1,0:T(1,128)} %reshape.570), calls=%async_computation.1 | async-start | bytes 393216 | tf_op jit(solution)/shard_map/all_to_all | solution.py:122
  102.6 13.3 %collective-permute-start.2 = (f32[3,15,128]{2,1,0:T(8,128)S(1)}, f32[3,15,128]{2,1,0:T(8,128)S(1)}, u32[]{:S(2)}, u32[]{:S(2)}) collective-permute-start(f32[3,15,128]{2,1,0:T(8,128)S(1)} %copy-done.83), channel_id=1, source_target_pairs={{0,31},{1,0},{2,1},{3,2},{4,3},{5,4},{6,5},{7,6},{8,7},{9,8},{10,9... | collective-permute-start | bytes 69128 | tf_op jit(solution)/shard_map/ppermute | solution.py:20
  116.2 10.2 %collective-permute-start.3 = (f32[3,15,128]{2,1,0:T(8,128)S(1)}, f32[3,15,128]{2,1,0:T(8,128)S(1)}, u32[]{:S(2)}, u32[]{:S(2)}) collective-permute-start(f32[3,15,128]{2,1,0:T(8,128)S(1)} %fusion.86), channel_id=1, source_target_pairs={{0,1},{1,2},{2,3},{3,4},{4,5},{5,6},{6,7},{7,8},{8,9},{9,10},{10,1... | collective-permute-start | bytes 69128 | tf_op jit(solution)/shard_map/ppermute | solution.py:20
  160.1 30.4 %collective-permute-start.4 = (f32[3,15,128]{2,1,0:T(8,128)}, f32[3,15,128]{2,1,0:T(8,128)S(1)}, u32[]{:S(2)}, u32[]{:S(2)}) collective-permute-start(f32[3,15,128]{2,1,0:T(8,128)} %slice.206), channel_id=1, source_target_pairs={{0,31},{1,0},{2,1},{3,2},{4,3},{5,4},{6,5},{7,6},{8,7},{9,8},{10,9... | collective-permute-start | bytes 69128 | tf_op jit(solution)/shard_map/ppermute | solution.py:20
  173.8 20.9 %copy-start.39 = (f32[3,3072]{1,0:T(4,128)S(1)}, f32[3,3072]{1,0:T(4,128)}, u32[]{:S(2)}) copy-start(f32[3,3072]{1,0:T(4,128)} %copy-done.38) | copy-start | bytes 110596
  173.8 20.9 %copy-start.55 = (f32[1,3072]{1,0:T(1,128)S(1)}, f32[1,3072]{1,0:T(1,128)}, u32[]{:S(2)}) copy-start(f32[1,3072]{1,0:T(1,128)} %copy-done.54) | copy-start | bytes 36868
  173.8 20.9 %copy-start.62 = (pred[3072]{0:T(1024)(128)(4,1)S(1)}, pred[3072]{0:T(1024)(128)(4,1)}, u32[]{:S(2)}) copy-start(pred[3072]{0:T(1024)(128)(4,1)} %copy-done.60) | copy-start | bytes 9220
  173.8 20.9 %copy-start.67 = (pred[3072]{0:T(1024)(128)(4,1)S(1)}, pred[3072]{0:T(1024)(128)(4,1)}, u32[]{:S(2)}) copy-start(pred[3072]{0:T(1024)(128)(4,1)} %copy-done.65) | copy-start | bytes 9220
  180.7 24.2 %all-to-all-start.2 = ((f32[128,1,360]{2,1,0:T(1,128)}), f32[128,1,360]{2,1,0:T(1,128)}, u32[]{:S(2)}, u32[]{:S(2)}) async-start(f32[128,1,360]{2,1,0:T(1,128)} %reshape.572), calls=%async_computation.2 | async-start | bytes 393216 | tf_op jit(solution)/shard_map/all_to_all | solution.py:122
  193.0 11.3 %collective-permute-start.5 = (f32[3,15,128]{2,1,0:T(8,128)S(1)}, f32[3,15,128]{2,1,0:T(8,128)S(1)}, u32[]{:S(2)}, u32[]{:S(2)}) collective-permute-start(f32[3,15,128]{2,1,0:T(8,128)S(1)} %fusion.85), channel_id=1, source_target_pairs={{0,1},{1,2},{2,3},{3,4},{4,5},{5,6},{6,7},{7,8},{8,9},{9,10},{10,1... | collective-permute-start | bytes 69128 | tf_op jit(solution)/shard_map/ppermute | solution.py:20
  243.3 27.3 %collective-permute-start.6 = (f32[3,15,128]{2,1,0:T(8,128)}, f32[3,15,128]{2,1,0:T(8,128)}, u32[]{:S(2)}, u32[]{:S(2)}) collective-permute-start(f32[3,15,128]{2,1,0:T(8,128)} %slice.211), channel_id=1, source_target_pairs={{0,31},{1,0},{2,1},{3,2},{4,3},{5,4},{6,5},{7,6},{8,7},{9,8},{10,9... | collective-permute-start | bytes 69128 | tf_op jit(solution)/shard_map/ppermute | solution.py:20
  253.6 18.5 %copy-start.97 = (pred[128]{0:T(512)(128)(4,1)S(1)}, pred[128]{0:T(512)(128)(4,1)}, u32[]{:S(2)}) copy-start(pred[128]{0:T(512)(128)(4,1)} %copy-done.95) | copy-start | bytes 388
  253.6 21.2 %copy-start.37 = (f32[2,8,24,128]{3,1,2,0:T(8,128)S(1)}, f32[2,8,24,128]{3,1,2,0:T(8,128)}, u32[]{:S(2)}) copy-start(f32[2,8,24,128]{3,1,2,0:T(8,128)} %copy.294) | copy-start | bytes 589828
  253.6 21.2 %copy-start.40 = (f32[3,3072]{1,0:T(4,128)S(1)}, f32[3,3072]{1,0:T(4,128)}, u32[]{:S(2)}) copy-start(f32[3,3072]{1,0:T(4,128)} %copy-done.38) | copy-start | bytes 110596
  253.7 21.1 %copy-start.56 = (f32[1,3072]{1,0:T(1,128)S(1)}, f32[1,3072]{1,0:T(1,128)}, u32[]{:S(2)}) copy-start(f32[1,3072]{1,0:T(1,128)} %copy-done.54) | copy-start | bytes 36868
  253.7 21.1 %copy-start.63 = (pred[3072]{0:T(1024)(128)(4,1)S(1)}, pred[3072]{0:T(1024)(128)(4,1)}, u32[]{:S(2)}) copy-start(pred[3072]{0:T(1024)(128)(4,1)} %copy-done.60) | copy-start | bytes 9220
  253.7 21.1 %copy-start.68 = (pred[3072]{0:T(1024)(128)(4,1)S(1)}, pred[3072]{0:T(1024)(128)(4,1)}, u32[]{:S(2)}) copy-start(pred[3072]{0:T(1024)(128)(4,1)} %copy-done.65) | copy-start | bytes 9220
  260.3 24.6 %all-to-all-start.3 = ((f32[128,1,360]{2,1,0:T(1,128)}), f32[128,1,360]{2,1,0:T(1,128)}, u32[]{:S(2)}, u32[]{:S(2)}) async-start(f32[128,1,360]{2,1,0:T(1,128)} %reshape.574), calls=%async_computation.3 | async-start | bytes 393216 | tf_op jit(solution)/shard_map/all_to_all | solution.py:122
  273.1 11.2 %collective-permute-start.7 = (f32[3,15,128]{2,1,0:T(8,128)S(1)}, f32[3,15,128]{2,1,0:T(8,128)S(1)}, u32[]{:S(2)}, u32[]{:S(2)}) collective-permute-start(f32[3,15,128]{2,1,0:T(8,128)S(1)} %fusion.84), channel_id=1, source_target_pairs={{0,1},{1,2},{2,3},{3,4},{4,5},{5,6},{6,7},{7,8},{8,9},{9,10},{10,1... | collective-permute-start | bytes 69128 | tf_op jit(solution)/shard_map/ppermute | solution.py:20
  313.0 18.3 %collective-permute-start.8 = (f32[3,15,128]{2,1,0:T(8,128)S(1)}, f32[3,15,128]{2,1,0:T(8,128)S(1)}, u32[]{:S(2)}, u32[]{:S(2)}) collective-permute-start(f32[3,15,128]{2,1,0:T(8,128)S(1)} %copy-done.82), channel_id=1, source_target_pairs={{0,31},{1,0},{2,1},{3,2},{4,3},{5,4},{6,5},{7,6},{8,7},{9,8},{10,9... | collective-permute-start | bytes 69128 | tf_op jit(solution)/shard_map/ppermute | solution.py:20
  321.4 20.5 %all-to-all-start.4 = ((f32[128,1,360]{2,1,0:T(1,128)}), f32[128,1,360]{2,1,0:T(1,128)S(1)}, u32[]{:S(2)}, u32[]{:S(2)}) async-start(f32[128,1,360]{2,1,0:T(1,128)} %reshape.576), calls=%async_computation.4 | async-start | bytes 393216 | tf_op jit(solution)/shard_map/all_to_all | solution.py:122
  331.5 6.3 %collective-permute-start.9 = (f32[3,15,128]{2,1,0:T(8,128)S(1)}, f32[3,15,128]{2,1,0:T(8,128)S(1)}, u32[]{:S(2)}, u32[]{:S(2)}) collective-permute-start(f32[3,15,128]{2,1,0:T(8,128)S(1)} %fusion.83), channel_id=1, source_target_pairs={{0,1},{1,2},{2,3},{3,4},{4,5},{5,6},{6,7},{7,8},{8,9},{9,10},{10,1... | collective-permute-start | bytes 69128 | tf_op jit(solution)/shard_map/ppermute | solution.py:20
  (92 other events, 581.1 us)
where the time goes:
time: 360 us; the launch traced here: 354 us
  local copies, waits for them, and re-layouts  152 us (42%)
  matrix products  88.5 us (25%)
  starting transfers between devices  67.4 us (19%)
  other arithmetic  39 us (11%)
    all_to_all x5, starting transfers between devices, shards(): lax.all_to_all(placed, ('group', 'sub'), split_axis=2, concat_axis=2, til...  54.5 us
    unnamed x243, local copies, waits for them, and re-layouts  41.7 us
    dot_general x15, matrix products, apply_mass(): spread = jnp.einsum('ij,cjf->cif', face_mass, traction, precision=highest)  19.3 us
    reshape x10, local copies, waits for them, and re-layouts, shards(): local_force.reshape(components, face_nodes, 3, elements)  16.9 us
    dot_general x5, matrix products, shards(): jnp.dot(strain_map.T, weighted, precision=highest)  15.6 us
    dot_general x5, matrix products, shards(): jnp.dot(strain_map, field.reshape(components * node_count, elements), pre...  14.3 us
    ppermute x10, starting transfers between devices, shifted(): return lax.ppermute(value, axis, pairs)  12.8 us
    dot_general x5, matrix products, shards(): jnp.einsum('cikjb,jkbql->ciqjl', own_local.reshape(components, face_nodes...  12.5 us
  transfers between devices with their start and end apart: 15, of which 1 were waited for; matrix products, arithmetic and copies ran while one was open for 35% of the time, Pallas kernels for 0%

commit v1 on v0

v1 whole, which is shorter than its diff:
```python
import functools

import jax
import jax.numpy as jnp
import numpy as np
from jax import lax
from jax.experimental import pallas as pl
from jax.experimental.pallas import tpu as pltpu
from jax.sharding import PartitionSpec as P

MESH = pl.DeviceIdType.MESH
HIGHEST = lax.Precision.HIGHEST
F32 = jnp.float32
BF16 = jnp.bfloat16

DT = 0.25
NODES = 35
FN = 15
LANES = 128
ROWS = 112
RIM = 48
REST = NODES - FN
PIECES = 6
GROUPS = 4
SUBS = 32
SLOT = 8
ROUNDS = 3


def row_of(c, n):
    return 16 * c + n if n < FN else RIM + REST * c + n - FN


def tables():
    points = [(a, b, c, 4 - a - b - c) for a in range(5) for b in range(5 - a) for c in range(5 - a - b)]
    faces = [[i for i, p in enumerate(points) if p[k] == 0] for k in range(4)]
    spread = np.zeros((ROWS, NODES), np.float32)
    perm = np.zeros((3 * NODES, ROWS), np.float32)
    select = np.zeros((4 * RIM, ROWS), np.float32)
    place = np.zeros((FN, 4 * RIM), np.float32)
    comp = np.full((ROWS,), -1, np.int64)
    for c in range(3):
        for n in range(NODES):
            spread[row_of(c, n), n] = 1.0
            perm[c * NODES + n, row_of(c, n)] = 1.0
            comp[row_of(c, n)] = c
        for k in range(4):
            for i, n in enumerate(faces[k]):
                select[k * RIM + 16 * c + i, row_of(c, n)] = 1.0
                place[i, k * RIM + 16 * c + i] = 1.0
    same = ((comp[:, None] == comp[None, :]) & (comp[:, None] >= 0)).astype(np.float32)
    block = np.arange(4 * RIM) // 16
    same_face = (block[:, None] == block[None, :]).astype(np.float32)
    return spread, perm, select, place, same, same_face


def dot(a, b, dims=((1,), (0,))):
    return lax.dot_general(a, b, (dims, ((), ())), precision=HIGHEST, preferred_element_type=F32)


def halves(x):
    high = x.astype(BF16)
    return high, (x - high.astype(F32)).astype(BF16)


def traction(j, u, rigid, soft):
    jn = u[0] * j[0] + u[1] * j[1] + u[2] * j[2]
    size = j[0] * j[0] + j[1] * j[1] + j[2] * j[2] + jn * jn
    e = soft * jnp.exp(size * -0.125)
    a = rigid + e
    b = e * jn
    return [a * j[c] + b * u[c] for c in range(3)]


def kernel(
    d_ref, v_ref, w_ref, jac_ref, s_ref, fm_ref, mi_ref, ll_ref, lg_ref, nl_ref, ng_ref, cl_ref, cg_ref,
    spread_ref, perm_ref, select_ref, place_ref, same_ref, face_ref,
    od_ref, ov_ref,
    f, v, fp, p, tp, amat, lmat, zmat, wj, ratio, lc, li, zc,
    xs, xr, ns, nr, xs_sem, xr_sem, ns_sem, nr_sem,
):
    g = lax.axis_index("group")
    s = lax.axis_index("sub")
    elements = f.shape[1]
    up = lax.rem(s + 1, SUBS)
    down = lax.rem(s + SUBS - 1, SUBS)
    barrier = pltpu.get_barrier_semaphore()

    def greet(t, carry):
        for b in range(GROUPS - 1):
            pl.semaphore_signal(
                barrier, inc=1, device_id=(lax.rem(g + 1 + b, GROUPS), t), device_id_type=MESH
            )
        return carry

    lax.fori_loop(0, SUBS, greet, 0)
    for t in (up, down):
        pl.semaphore_signal(barrier, inc=1, device_id=(g, t), device_id_type=MESH)

    jac = jac_ref[...].reshape(1, elements)
    inv = 1.0 / jac
    wj[...] = w_ref[...] * (inv * -DT)
    for q in range(3):
        part = pl.ds(q * elements, elements)
        state = ll_ref[1:2, part]
        scale = lg_ref[3:4, part] * (inv * DT)
        lc[q, 0:3, :] = lg_ref[0:3, part]
        lc[q, 3:4, :] = jnp.where(state == 0, scale, 0.0)
        lc[q, 4:5, :] = jnp.where(state == 1, 0.5 * scale, 0.0)
        partner = ll_ref[0:1, part]
        li[q, 0:1, :] = lax.rem(partner, LANES)
        li[q, 1:2, :] = lax.div(partner, LANES)
    cross = elements - 2 * LANES
    spots = (
        (0, LANES, ng_ref[0:4, :], nl_ref[0:1, :]),
        (LANES, LANES, ng_ref[4:8, :], nl_ref[1:2, :]),
        (2 * LANES, cross, cg_ref[...], cl_ref[...].reshape(1, cross)),
    )
    for at, size, geometry, state in spots:
        lanes = pl.ds(at, size)
        scale = geometry[3:4, :] * (inv[:, at : at + size] * DT)
        zc[0:3, lanes] = geometry[0:3, :]
        zc[3:4, lanes] = jnp.where(state == 0, scale, 0.0)
        zc[4:5, lanes] = jnp.where(state == 1, 0.5 * scale, 0.0)

    for source, target in ((d_ref, f), (v_ref, v)):
        for c in range(3):
            target[16 * c : 16 * c + FN, :] = source[c, 0:FN, :]
            target[16 * c + FN : 16 * c + FN + 1, :] = jnp.zeros((1, elements), F32)
            target[RIM + REST * c : RIM + REST * (c + 1), :] = source[c, FN:NODES, :]
        target[RIM + 3 * REST :, :] = jnp.zeros((ROWS - RIM - 3 * REST, elements), F32)
    f[FN : FN + 1, :] = inv

    spread = spread_ref[...]
    mass = dot(dot(spread, mi_ref[...]), spread, ((1,), (1,))) * same_ref[...]
    place = place_ref[...]
    face = dot(dot(place, fm_ref[...], ((0,), (0,))), place) * face_ref[...]
    lift = dot(mass, dot(select_ref[...], face, ((0,), (0,))))
    high, low = halves(lift)
    zmat[:, 0:RIM] = high[:, 0:RIM]
    zmat[:, RIM : 2 * RIM] = high[:, 0:RIM]
    zmat[:, 2 * RIM : 3 * RIM] = low[:, 0:RIM]
    lmat[:, 0 : 3 * RIM] = high[:, RIM:]
    lmat[:, 3 * RIM : 6 * RIM] = high[:, RIM:]
    lmat[:, 6 * RIM : 9 * RIM] = low[:, RIM:]
    for m in range(PIECES):
        piece = dot(s_ref[m * 3 * NODES : (m + 1) * 3 * NODES, :], perm_ref[...])
        high, low = halves(dot(mass, dot(piece, piece, ((0,), (0,)))))
        rows = slice(m * ROWS, (m + 1) * ROWS)
        amat[rows, 0:ROWS] = high
        amat[rows, ROWS : 2 * ROWS] = high
        amat[rows, 2 * ROWS : 3 * ROWS] = low
    chosen = select_ref[RIM:, :].astype(BF16)
    rows = slice(PIECES * ROWS, PIECES * ROWS + 3 * RIM)
    amat[rows, 0:ROWS] = chosen
    amat[rows, ROWS : 2 * ROWS] = chosen
    amat[rows, 2 * ROWS : 3 * ROWS] = jnp.zeros((3 * RIM, ROWS), BF16)

    def local(width=2 * LANES):
        for at in range(0, elements, width):
            lanes = pl.ds(at, width)
            old = f[:, lanes]
            high, low = halves(old)
            product = jnp.dot(
                amat[...], jnp.concatenate([high, low, high], axis=0), preferred_element_type=F32
            )
            change = wj[0:1, lanes] * product[0:ROWS, :]
            for m in range(1, PIECES):
                change = change + wj[m : m + 1, lanes] * product[m * ROWS : (m + 1) * ROWS, :]
            highs, lows = [], []
            trace = [product[PIECES * ROWS + q * RIM : PIECES * ROWS + (q + 1) * RIM, :] for q in range(3)]
            for q in range(3):
                pulls = []
                for block in range(0, width, LANES):
                    here = slice(block, block + LANES)
                    index = jnp.broadcast_to(li[q, 0:1, pl.ds(at + block, LANES)], (RIM, LANES))
                    origin = jnp.broadcast_to(li[q, 1:2, pl.ds(at + block, LANES)], (RIM, LANES))
                    found = [
                        jnp.take_along_axis(trace[r][:, here], index, axis=1, mode="promise_in_bounds")
                        for r in range(3)
                    ]
                    paired = jnp.where(origin == 0, found[0], jnp.where(origin == 1, found[1], found[2]))
                    jump = paired - trace[q][:, here]
                    at_lanes = pl.ds(at + block, LANES)
                    pulls.append(
                        jnp.concatenate(
                            traction(
                                [jump[16 * c : 16 * (c + 1), :] for c in range(3)],
                                [lc[q, c : c + 1, at_lanes] for c in range(3)],
                                lc[q, 3:4, at_lanes],
                                lc[q, 4:5, at_lanes],
                            ),
                            axis=0,
                        )
                    )
                high, low = halves(jnp.concatenate(pulls, axis=1))
                highs.append(high)
                lows.append(low)
            change = change + jnp.dot(
                lmat[...], jnp.concatenate(highs + lows + highs, axis=0), preferred_element_type=F32
            )
            speed = v[:, lanes] + change
            v[:, lanes] = speed
            fp[:, lanes] = old + DT * speed

    def rim(advance, width=2 * LANES):
        for at in range(0, elements, width):
            lanes = pl.ds(at, width)
            jump = p[:, lanes] - f[0:RIM, lanes]
            pull = jnp.concatenate(
                traction(
                    [jump[16 * c : 16 * (c + 1), :] for c in range(3)],
                    [zc[c : c + 1, lanes] for c in range(3)],
                    zc[3:4, lanes],
                    zc[4:5, lanes],
                ),
                axis=0,
            )
            high, low = halves(pull)
            change = jnp.dot(
                zmat[...], jnp.concatenate([high, low, high], axis=0), preferred_element_type=F32
            )
            v[:, lanes] = v[:, lanes] + change
            f[:, lanes] = fp[:, lanes] + DT * change
            if advance:
                p[:, lanes] = tp[:, lanes] - (DT * ratio[0:1, lanes]) * change[0:RIM, :]

    def cross_copy(turn, b, t):
        return pltpu.make_async_remote_copy(
            src_ref=xs.at[turn, b * SUBS + t],
            dst_ref=xr.at[turn, (GROUPS - 2 - b) * SUBS + s],
            send_sem=xs_sem.at[turn],
            recv_sem=xr_sem.at[turn],
            device_id=(lax.rem(g + 1 + b, GROUPS), t),
            device_id_type=MESH,
        )

    def side_copy(turn, side):
        return pltpu.make_async_remote_copy(
            src_ref=ns.at[turn, side],
            dst_ref=nr.at[turn, 1 - side],
            send_sem=ns_sem.at[turn, side],
            recv_sem=nr_sem.at[turn, 1 - side],
            device_id=(g, down if side else up),
            device_id_type=MESH,
        )

    blank = jnp.zeros((LANES - 2 * RIM, LANES), F32)

    def send(turn):
        for block in range((GROUPS - 1) * SUBS * SLOT // LANES):
            lanes = pl.ds((2 + block) * LANES, LANES)
            tile = jnp.concatenate([f[0:RIM, lanes], fp[0:RIM, lanes], blank], axis=0)
            per = LANES // SLOT
            xs[turn, block * per : (block + 1) * per, :, :] = tile.T.reshape(per, SLOT, LANES)
        for side in range(2):
            lanes = pl.ds(side * LANES, LANES)
            ns[turn, side, 0:RIM, :] = f[0:RIM, lanes]
            ns[turn, side, RIM:, :] = fp[0:RIM, lanes]

        def go(k, carry):
            t = lax.rem(s + k, SUBS)
            for b in range(GROUPS - 1):
                cross_copy(turn, b, t).start()
            return carry

        lax.fori_loop(0, SUBS, go, 0)
        for side in range(2):
            side_copy(turn, side).start()

    def receive(turn):
        for side in range(2):
            side_copy(turn, 1 - side).wait_recv()
            lanes = pl.ds(side * LANES, LANES)
            p[:, lanes] = nr[turn, side, 0:RIM, :]
            tp[:, lanes] = nr[turn, side, RIM:, :]
        pltpu.make_async_copy(xr.at[turn], xr.at[turn], xr_sem.at[turn]).wait()
        for block in range((GROUPS - 1) * SUBS * SLOT // LANES):
            lanes = pl.ds((2 + block) * LANES, LANES)
            per = LANES // SLOT
            tile = xr[turn, block * per : (block + 1) * per, :, :].reshape(LANES, LANES).T
            p[:, lanes] = tile[0:RIM, :]
            tp[:, lanes] = tile[RIM : 2 * RIM, :]

    local()
    pl.semaphore_wait(barrier, (GROUPS - 1) * SUBS + 2)

    def pair(turn, carry):
        @pl.when(turn > 0)
        def _():
            local()

        send(turn)
        receive(turn)
        ratio[...] = p[FN : FN + 1, :] * jac_ref[...].reshape(1, elements)
        rim(True)
        local()
        rim(False)
        return carry

    lax.fori_loop(0, ROUNDS - 1, pair, 0)
    send(ROUNDS - 1)
    local()
    receive(ROUNDS - 1)
    rim(False)

    for source, target in ((f, od_ref), (v, ov_ref)):
        for c in range(3):
            target[c, 0:FN, :] = source[16 * c : 16 * c + FN, :]
            target[c, FN:NODES, :] = source[RIM + REST * c : RIM + REST * (c + 1), :]
    for turn in range(ROUNDS):
        pltpu.make_async_copy(xs.at[turn], xs.at[turn], xs_sem.at[turn]).wait()
        for side in range(2):
            side_copy(turn, side).wait_send()


def shards(*args):
    elements = args[0].shape[2]
    consts = tuple(jnp.asarray(t) for t in tables())
    shape = jax.ShapeDtypeStruct(args[0].shape, F32)
    slots = (GROUPS - 1) * SUBS
    vmem = pl.BlockSpec(memory_space=pltpu.VMEM)
    return pl.pallas_call(
        kernel,
        out_shape=(shape, shape),
        in_specs=[vmem] * (len(args) + len(consts)),
        out_specs=(vmem, vmem),
        scratch_shapes=[
            pltpu.VMEM((ROWS, elements), F32),
            pltpu.VMEM((ROWS, elements), F32),
            pltpu.VMEM((ROWS, elements), F32),
            pltpu.VMEM((RIM, elements), F32),
            pltpu.VMEM((RIM, elements), F32),
            pltpu.VMEM((PIECES * ROWS + 3 * RIM, 3 * ROWS), BF16),
            pltpu.VMEM((ROWS, 9 * RIM), BF16),
            pltpu.VMEM((ROWS, 3 * RIM), BF16),
            pltpu.VMEM((PIECES, elements), F32),
            pltpu.VMEM((1, elements), F32),
            pltpu.VMEM((3, 5, elements), F32),
            pltpu.VMEM((3, 2, elements), jnp.int32),
            pltpu.VMEM((5, elements), F32),
            pltpu.VMEM((ROUNDS, slots, SLOT, LANES), F32),
            pltpu.VMEM((ROUNDS, slots, SLOT, LANES), F32),
            pltpu.VMEM((ROUNDS, 2, 2 * RIM, LANES), F32),
            pltpu.VMEM((ROUNDS, 2, 2 * RIM, LANES), F32),
            pltpu.SemaphoreType.DMA((ROUNDS,)),
            pltpu.SemaphoreType.DMA((ROUNDS,)),
            pltpu.SemaphoreType.DMA((ROUNDS, 2)),
            pltpu.SemaphoreType.DMA((ROUNDS, 2)),
        ],
        compiler_params=pltpu.CompilerParams(collective_id=0, has_side_effects=True),
    )(*args, *consts)


def solution(mesh):
    lanes = P(None, ("group", "sub"))
    state = P(None, None, ("group", "sub"))
    flat = P(("group", "sub"))
    return jax.shard_map(
        shards,
        mesh=mesh,
        in_specs=(state, state, lanes, flat, P(), P(), P(), lanes, lanes, lanes, lanes, flat, lanes),
        out_specs=(state, state),
        check_vma=False,
    )
```

time: 360 us -> 60.9 us (0.17); the launches traced: 354 us -> 60.7 us
  local copies, waits for them, and re-layouts: 152 us -> 4.55 us
  matrix products: 88.5 us -> 0 us
  starting transfers between devices: 67.4 us -> 0 us
  Pallas kernels: 0 us -> 55.5 us
  other arithmetic: 39 us -> 0 us
    dot_general x45 -> x0, matrix products: 88.5 us -> none  [the longest x15 19.3 us: apply_mass(): spread = jnp.einsum('ij,cjf->cif', face_mass, traction, precision=highest)]
    reshape x51 -> x0, local copies, waits for them, and re-layouts: 74.5 us -> none  [the longest x10 16.9 us: shards(): local_force.reshape(components, face_nodes, 3, elements)]
    pallas_call x0 -> x1, Pallas kernels: none -> 55.5 us  [shards(): pl.pallas_call(kernel, out_shape=(shape, shape), in_specs=[vmem] * (len(a...]
    all_to_all x5 -> x0, starting transfers between devices: 54.5 us -> none  [shards(): lax.all_to_all(placed, ('group', 'sub'), split_axis=2, concat_axis=2, til...]
    unnamed x243 -> x5, local copies, waits for them, and re-layouts: 41.7 us -> 4.55 us
    slice x28 -> x0, local copies, waits for them, and re-layouts: 14 us -> none  [the longest x10 9.17 us: shards(): own_local = traces[:, :, 1:]]
    ppermute x10 -> x0, starting transfers between devices: 12.8 us -> none  [shifted(): return lax.ppermute(value, axis, pairs)]
    all_to_all x5 -> x0, other arithmetic: 9.84 us -> none  [shards(): lax.all_to_all(placed, ('group', 'sub'), split_axis=2, concat_axis=2, til...]
  transfers between devices with their start and end apart: 15 -> 0, of which waited for: 1 -> 0; matrix products, arithmetic and copies ran while one was open for 35% -> 0% of each run, Pallas kernels for 0% -> 0%
where the time goes in v1:
time: 60.9 us; the launch traced here: 60.7 us
  Pallas kernels  55.5 us (91%)
  local copies, waits for them, and re-layouts  4.55 us (7%)
  between operations  0.65 us (1%)
    pallas_call x1, Pallas kernels, shards(): pl.pallas_call(kernel, out_shape=(shape, shape), in_specs=[vmem] * (len(a...  55.5 us
    unnamed x5, local copies, waits for them, and re-layouts  4.55 us

profile of v1, /device:TPU:1, one launch (start us, length us, event | category | flops | bytes accessed | tf_op | source)
XLA Modules:
  0.0 60.7 jit_solution(3055855750839209352)
XLA Ops:
  0.6 1.9 %copy.21.s_ref = f32[630,105]{1,0:T(8,128)} copy(f32[630,105]{0,1:T(8,128)} %param.23) | data formatting | bytes 529200 | tf_op args[4]
  2.5 55.5 %shard_map.194 = (f32[3,35,1024]{2,1,0:T(8,128)}, f32[3,35,1024]{2,1,0:T(8,128)}) custom-call(f32[3,35,1024]{2,1,0:T(8,128)} %d_ref.1, f32[3,35,1024]{2,1,0:T(8,128)} %v_ref.1, f32[6,1024]{1,0:T(8,128)} %w_ref.1, f32[1024]{0:T(1024)} %jac_ref.1, f32[630,105]{1,0:T(8,128)} %copy.21.s_ref, f32[15,15]{1,0:T(8,128)} %fm_ref.1, f32[35,35]{1,0:T(8,128)} %mi_ref.1, ...), custom_call_target="tpu_custom_call" | custom-call | tf_op jit(solution)/shard_map/pallas_call | solution.py:323
  58.0 0.0 copy-start
  58.0 1.9 %copy.24 = f32[3,35,1024]{2,1,0:T(8,128)} copy(f32[3,35,1024]{2,1,0:T(8,128)} %get-tuple-element.4) | data formatting | bytes 860160
  59.9 0.0 copy-done
  59.9 0.8 %copy.25 = f32[3,35,1024]{2,1,0:T(8,128)} copy(f32[3,35,1024]{2,1,0:T(8,128)S(1)} %copy-done) | data formatting | bytes 860160
Async XLA Ops:
  58.0 1.9 %copy-start = (f32[3,35,1024]{2,1,0:T(8,128)S(1)}, f32[3,35,1024]{2,1,0:T(8,128)}, u32[]{:S(2)}) copy-start(f32[3,35,1024]{2,1,0:T(8,128)} %get-tuple-element.5) | copy-start | bytes 1290244

commit v2 on v1

--- a/solution.py
+++ b/solution.py
@@ -76,7 +76,7 @@
     d_ref, v_ref, w_ref, jac_ref, s_ref, fm_ref, mi_ref, ll_ref, lg_ref, nl_ref, ng_ref, cl_ref, cg_ref,
     spread_ref, perm_ref, select_ref, place_ref, same_ref, face_ref,
     od_ref, ov_ref,
-    f, v, fp, p, tp, amat, lmat, zmat, wj, ratio, lc, li, zc,
+    f, v, fp, p, tp, amat, smat, lmat, zmat, fh, tr, th, wj, ratio, lc, li, zc,
     xs, xr, ns, nr, xs_sem, xr_sem, ns_sem, nr_sem,
 ):
     g = lax.axis_index("group")
@@ -143,65 +143,65 @@
     lmat[:, 0 : 3 * RIM] = high[:, RIM:]
     lmat[:, 3 * RIM : 6 * RIM] = high[:, RIM:]
     lmat[:, 6 * RIM : 9 * RIM] = low[:, RIM:]
+    turned = dot(perm_ref[...], s_ref[...], ((0,), (0,)))
     for m in range(PIECES):
-        piece = dot(s_ref[m * 3 * NODES : (m + 1) * 3 * NODES, :], perm_ref[...])
-        high, low = halves(dot(mass, dot(piece, piece, ((0,), (0,)))))
+        piece = turned[:, m * 3 * NODES : (m + 1) * 3 * NODES]
+        high, low = halves(dot(mass, dot(piece, piece, ((1,), (1,)))))
         rows = slice(m * ROWS, (m + 1) * ROWS)
         amat[rows, 0:ROWS] = high
         amat[rows, ROWS : 2 * ROWS] = high
         amat[rows, 2 * ROWS : 3 * ROWS] = low
     chosen = select_ref[RIM:, :].astype(BF16)
-    rows = slice(PIECES * ROWS, PIECES * ROWS + 3 * RIM)
-    amat[rows, 0:ROWS] = chosen
-    amat[rows, ROWS : 2 * ROWS] = chosen
-    amat[rows, 2 * ROWS : 3 * ROWS] = jnp.zeros((3 * RIM, ROWS), BF16)
+    smat[:, 0:ROWS] = chosen
+    smat[:, ROWS : 2 * ROWS] = chosen
 
     def local(width=2 * LANES):
         for at in range(0, elements, width):
             lanes = pl.ds(at, width)
-            old = f[:, lanes]
-            high, low = halves(old)
-            product = jnp.dot(
-                amat[...], jnp.concatenate([high, low, high], axis=0), preferred_element_type=F32
-            )
+            high, low = halves(f[:, lanes])
+            fh[0:ROWS, lanes] = high
+            fh[ROWS : 2 * ROWS, lanes] = low
+            fh[2 * ROWS :, lanes] = high
+            tr[:, lanes] = jnp.dot(smat[...], fh[0 : 2 * ROWS, lanes], preferred_element_type=F32)
+        for at in range(0, elements, width):
+            lanes = pl.ds(at, width)
+            product = jnp.dot(amat[...], fh[:, lanes], preferred_element_type=F32)
             change = wj[0:1, lanes] * product[0:ROWS, :]
             for m in range(1, PIECES):
                 change = change + wj[m : m + 1, lanes] * product[m * ROWS : (m + 1) * ROWS, :]
-            highs, lows = [], []
-            trace = [product[PIECES * ROWS + q * RIM : PIECES * ROWS + (q + 1) * RIM, :] for q in range(3)]
-            for q in range(3):
-                pulls = []
-                for block in range(0, width, LANES):
-                    here = slice(block, block + LANES)
-                    index = jnp.broadcast_to(li[q, 0:1, pl.ds(at + block, LANES)], (RIM, LANES))
-                    origin = jnp.broadcast_to(li[q, 1:2, pl.ds(at + block, LANES)], (RIM, LANES))
-                    found = [
-                        jnp.take_along_axis(trace[r][:, here], index, axis=1, mode="promise_in_bounds")
-                        for r in range(3)
-                    ]
-                    paired = jnp.where(origin == 0, found[0], jnp.where(origin == 1, found[1], found[2]))
-                    jump = paired - trace[q][:, here]
-                    at_lanes = pl.ds(at + block, LANES)
-                    pulls.append(
-                        jnp.concatenate(
-                            traction(
-                                [jump[16 * c : 16 * (c + 1), :] for c in range(3)],
-                                [lc[q, c : c + 1, at_lanes] for c in range(3)],
-                                lc[q, 3:4, at_lanes],
-                                lc[q, 4:5, at_lanes],
-                            ),
-                            axis=0,
-                        )
+            v[:, lanes] = v[:, lanes] + change
+            for block in range(at, at + width, LANES):
+                pull(block)
+        for at in range(0, elements, width):
+            lanes = pl.ds(at, width)
+            speed = v[:, lanes] + jnp.dot(lmat[...], th[:, lanes], preferred_element_type=F32)
+            v[:, lanes] = speed
+            fp[:, lanes] = f[:, lanes] + DT * speed
+
+    def pull(block):
+        here = pl.ds(block, LANES)
+        for q in range(3):
+            index = jnp.broadcast_to(li[q, 0:1, here], (16, LANES))
+            origin = jnp.broadcast_to(li[q, 1:2, here], (16, LANES))
+            jump = []
+            for c in range(3):
+                found = [
+                    jnp.take_along_axis(
+                        tr[r * RIM + 16 * c : r * RIM + 16 * (c + 1), here], index, axis=1, mode="promise_in_bounds"
                     )
-                high, low = halves(jnp.concatenate(pulls, axis=1))
-                highs.append(high)
-                lows.append(low)
-            change = change + jnp.dot(
-                lmat[...], jnp.concatenate(highs + lows + highs, axis=0), preferred_element_type=F32
+                    for r in range(3)
+                ]
+                paired = jnp.where(origin == 0, found[0], jnp.where(origin == 1, found[1], found[2]))
+                jump.append(paired - tr[q * RIM + 16 * c : q * RIM + 16 * (c + 1), here])
+            parts = traction(
+                jump, [lc[q, c : c + 1, here] for c in range(3)], lc[q, 3:4, here], lc[q, 4:5, here]
             )
-            speed = v[:, lanes] + change
-            v[:, lanes] = speed
-            fp[:, lanes] = old + DT * speed
+            for c in range(3):
+                high, low = halves(parts[c])
+                at = q * RIM + 16 * c
+                th[at : at + 16, here] = high
+                th[3 * RIM + at : 3 * RIM + at + 16, here] = low
+                th[6 * RIM + at : 6 * RIM + at + 16, here] = high
 
     def rim(advance, width=2 * LANES):
         for at in range(0, elements, width):
@@ -316,6 +316,7 @@
 
 def shards(*args):
     elements = args[0].shape[2]
+    args = args[:4] + (args[4].T,) + args[5:]
     consts = tuple(jnp.asarray(t) for t in tables())
     shape = jax.ShapeDtypeStruct(args[0].shape, F32)
     slots = (GROUPS - 1) * SUBS
@@ -331,9 +332,13 @@
             pltpu.VMEM((ROWS, elements), F32),
             pltpu.VMEM((RIM, elements), F32),
             pltpu.VMEM((RIM, elements), F32),
-            pltpu.VMEM((PIECES * ROWS + 3 * RIM, 3 * ROWS), BF16),
+            pltpu.VMEM((PIECES * ROWS, 3 * ROWS), BF16),
+            pltpu.VMEM((3 * RIM, 2 * ROWS), BF16),
             pltpu.VMEM((ROWS, 9 * RIM), BF16),
             pltpu.VMEM((ROWS, 3 * RIM), BF16),
+            pltpu.VMEM((3 * ROWS, elements), BF16),
+            pltpu.VMEM((3 * RIM, elements), F32),
+            pltpu.VMEM((9 * RIM, elements), BF16),
             pltpu.VMEM((PIECES, elements), F32),
             pltpu.VMEM((1, elements), F32),
             pltpu.VMEM((3, 5, elements), F32),

time: 60.9 us -> 49.8 us (0.82)
  Pallas kernels: 55.5 us -> 46.3 us
  local copies, waits for them, and re-layouts: 4.55 us -> 2.69 us
    pallas_call x1, Pallas kernels: 55.5 us -> 46.3 us  [shards(): pl.pallas_call(kernel, out_shape=(shape, shape), in_specs=[vmem] * (len(a...]
    unnamed x5 -> x4, local copies, waits for them, and re-layouts: 4.55 us -> 2.69 us
where the time goes in v2:
time: 49.8 us; the launch traced here: 49.6 us
  Pallas kernels  46.3 us (93%)
  local copies, waits for them, and re-layouts  2.69 us (5%)
  between operations  0.65 us (1%)
    pallas_call x1, Pallas kernels, shards(): pl.pallas_call(kernel, out_shape=(shape, shape), in_specs=[vmem] * (len(a...  46.3 us
    unnamed x4, local copies, waits for them, and re-layouts  2.69 us

profile of v2, /device:TPU:1, one launch (start us, length us, event | category | flops | bytes accessed | tf_op | source)
XLA Modules:
  0.0 49.6 jit_solution(5084480119275792929)
XLA Ops:
  0.6 46.3 %shard_map.194 = (f32[3,35,1024]{2,1,0:T(8,128)}, f32[3,35,1024]{2,1,0:T(8,128)}) custom-call(f32[3,35,1024]{2,1,0:T(8,128)} %d_ref.1, f32[3,35,1024]{2,1,0:T(8,128)} %v_ref.1, f32[6,1024]{1,0:T(8,128)} %w_ref.1, f32[1024]{0:T(1024)} %jac_ref.1, f32[105,630]{1,0:T(8,128)} %bitcast.1, f32[15,15]{1,0:T(8,128)} %fm_ref.1, f32[35,35]{1,0:T(8,128)} %mi_ref.1, ...), custom_call_target="tpu_custom_call" | custom-call | tf_op jit(solution)/shard_map/pallas_call | solution.py:324
  46.9 0.0 copy-start
  46.9 1.9 %copy.23 = f32[3,35,1024]{2,1,0:T(8,128)} copy(f32[3,35,1024]{2,1,0:T(8,128)} %get-tuple-element.4) | data formatting | bytes 860160
  48.8 0.0 copy-done
  48.8 0.8 %copy.24 = f32[3,35,1024]{2,1,0:T(8,128)} copy(f32[3,35,1024]{2,1,0:T(8,128)S(1)} %copy-done) | data formatting | bytes 860160
Async XLA Ops:
  46.9 1.9 %copy-start = (f32[3,35,1024]{2,1,0:T(8,128)S(1)}, f32[3,35,1024]{2,1,0:T(8,128)}, u32[]{:S(2)}) copy-start(f32[3,35,1024]{2,1,0:T(8,128)} %get-tuple-element.5) | copy-start | bytes 1290244

commit v3 on v2

--- a/solution.py
+++ b/solution.py
@@ -25,6 +25,13 @@
 SUBS = 32
 SLOT = 8
 ROUNDS = 3
+MESSAGES = 2 * ROUNDS - 1
+LINES = 3
+NAMES = (
+    "displacement", "velocity", "weights", "jacobian", "strain", "face_mass", "mass", "local_links", "local_geometry",
+    "side_links", "side_geometry", "cross_links", "cross_geometry",
+    "spread", "perm", "select", "place", "same", "face",
+)
 
 
 def row_of(c, n):
@@ -72,13 +79,20 @@
     return [a * j[c] + b * u[c] for c in range(3)]
 
 
-def kernel(
-    d_ref, v_ref, w_ref, jac_ref, s_ref, fm_ref, mi_ref, ll_ref, lg_ref, nl_ref, ng_ref, cl_ref, cg_ref,
-    spread_ref, perm_ref, select_ref, place_ref, same_ref, face_ref,
-    od_ref, ov_ref,
-    f, v, fp, p, tp, amat, smat, lmat, zmat, fh, tr, th, wj, ratio, lc, li, zc,
-    xs, xr, ns, nr, xs_sem, xr_sem, ns_sem, nr_sem,
-):
+def kernel(*refs):
+    count = len(NAMES)
+    hbm = refs[:count]
+    ovp, ofp, oc = refs[count : count + 3]
+    buffers = refs[count + 3 : 2 * count + 3]
+    (
+        f, v, fp, p, ch, amat, smat, lmat, zmat, fh, tr, th, wj, ratio, lc, li, zc,
+        xs, xr, ns, nr, in_sem, xs_sem, xr_sem, ns_sem, nr_sem,
+    ) = refs[2 * count + 3 :]
+    (
+        d_ref, v_ref, w_ref, jac_ref, s_ref, fm_ref, mi_ref, ll_ref, lg_ref, nl_ref, ng_ref, cl_ref, cg_ref,
+        spread_ref, perm_ref, select_ref, place_ref, same_ref, face_ref,
+    ) = buffers
+    loads = [pltpu.make_async_copy(hbm[k], buffers[k], in_sem.at[k]) for k in range(count)]
     g = lax.axis_index("group")
     s = lax.axis_index("sub")
     elements = f.shape[1]
@@ -96,9 +110,115 @@
     lax.fori_loop(0, SUBS, greet, 0)
     for t in (up, down):
         pl.semaphore_signal(barrier, inc=1, device_id=(g, t), device_id_type=MESH)
-
+    first = (NAMES.index("displacement"), NAMES.index("jacobian"))
+    for k in first:
+        loads[k].start()
+    for k in range(count):
+        if k not in first:
+            loads[k].start()
+
+    def fill(source, target):
+        for c in range(3):
+            target[16 * c : 16 * c + FN, :] = source[c, 0:FN, :]
+            target[16 * c + FN : 16 * c + FN + 1, :] = jnp.zeros((1, elements), F32)
+            target[RIM + REST * c : RIM + REST * (c + 1), :] = source[c, FN:NODES, :]
+        target[RIM + 3 * REST :, :] = jnp.zeros((ROWS - RIM - 3 * REST, elements), F32)
+
+    for k in first:
+        loads[k].wait()
     jac = jac_ref[...].reshape(1, elements)
     inv = 1.0 / jac
+    fill(d_ref, f)
+    f[FN : FN + 1, :] = inv
+
+    def cross_copy(turn, b, t):
+        return pltpu.make_async_remote_copy(
+            src_ref=xs.at[turn, b * SUBS + t],
+            dst_ref=xr.at[turn, (GROUPS - 2 - b) * SUBS + s],
+            send_sem=xs_sem.at[turn],
+            recv_sem=xr_sem.at[turn],
+            device_id=(lax.rem(g + 1 + b, GROUPS), t),
+            device_id_type=MESH,
+        )
+
+    def side_copy(turn, side):
+        return pltpu.make_async_remote_copy(
+            src_ref=ns.at[turn, side],
+            dst_ref=nr.at[turn, 1 - side],
+            send_sem=ns_sem.at[turn, side],
+            recv_sem=nr_sem.at[turn, 1 - side],
+            device_id=(g, down if side else up),
+            device_id_type=MESH,
+        )
+
+    per = LANES // SLOT
+    slot = lax.rem(lax.broadcasted_iota(jnp.int32, (8, LANES), 1), SLOT)
+
+    def shift(x, by):
+        return pltpu.roll(x, by % LANES, 1) if by % LANES else x
+
+    def pack(turn, source):
+        for block in range((GROUPS - 1) * SUBS // per):
+            lanes = pl.ds((2 + block) * LANES, LANES)
+            x = [source[8 * k : 8 * k + 8, lanes] for k in range(6)]
+            tile = x + [shift(x[k], -3) for k in range(6)]
+            for k in range(4):
+                parts = []
+                for r in range(3):
+                    i = 4 * r + k
+                    parts.append(shift(x[i % 6], r - (6 + i // 6)))
+                tile.append(jnp.where(slot == 0, parts[0], jnp.where(slot == 1, parts[1], parts[2])))
+            turned = jnp.concatenate(tile, axis=0).T.reshape(per, SLOT, LANES)
+            xs[turn, block * per : (block + 1) * per, :, :] = turned[:, 0:LINES, :]
+        for side in range(2):
+            ns[turn, side, :, :] = source[0:RIM, pl.ds(side * LANES, LANES)]
+
+    def send(turn):
+        def go(k, carry):
+            t = lax.rem(s + k, SUBS)
+            for b in range(GROUPS - 1):
+                cross_copy(turn, b, t).start()
+            return carry
+
+        lax.fori_loop(0, SUBS, go, 0)
+        for side in range(2):
+            side_copy(turn, side).start()
+
+    def receive(turn, target):
+        for side in range(2):
+            side_copy(turn, 1 - side).wait_recv()
+            target[:, pl.ds(side * LANES, LANES)] = nr[turn, side, :, :]
+        pltpu.make_async_copy(xr.at[turn], xr.at[turn], xr_sem.at[turn]).wait()
+        for block in range((GROUPS - 1) * SUBS // per):
+            lanes = pl.ds((2 + block) * LANES, LANES)
+            rows = xr[turn, block * per : (block + 1) * per, :, :]
+            rows = jnp.concatenate([rows, jnp.zeros((per, SLOT - LINES, LANES), F32)], axis=1)
+            tile = rows.reshape(LANES, LANES).T
+            for k in range(6):
+                x = tile[8 * k : 8 * k + 8, :]
+                y = shift(tile[RIM + 8 * k : RIM + 8 * k + 8, :], 3)
+                late = []
+                for q in range(2):
+                    i = 6 * q + k
+                    at = 2 * RIM + 8 * (i % 4)
+                    late.append(shift(tile[at : at + 8, :], 6 + q - i // 4))
+                y = jnp.where(slot < 6, y, jnp.where(slot == 6, late[0], late[1]))
+                target[8 * k : 8 * k + 8, lanes] = jnp.where(slot < 3, x, y)
+
+    def empty(source, target):
+        for c in range(3):
+            target[c, 0:FN, :] = source[16 * c : 16 * c + FN, :]
+            target[c, FN:NODES, :] = source[RIM + REST * c : RIM + REST * (c + 1), :]
+
+    pack(0, f)
+    pl.semaphore_wait(barrier, (GROUPS - 1) * SUBS + 2)
+    send(0)
+
+    for k in range(count):
+        if k not in first:
+            loads[k].wait()
+    fill(v_ref, v)
+
     wj[...] = w_ref[...] * (inv * -DT)
     for q in range(3):
         part = pl.ds(q * elements, elements)
@@ -122,14 +242,6 @@
         zc[0:3, lanes] = geometry[0:3, :]
         zc[3:4, lanes] = jnp.where(state == 0, scale, 0.0)
         zc[4:5, lanes] = jnp.where(state == 1, 0.5 * scale, 0.0)
-
-    for source, target in ((d_ref, f), (v_ref, v)):
-        for c in range(3):
-            target[16 * c : 16 * c + FN, :] = source[c, 0:FN, :]
-            target[16 * c + FN : 16 * c + FN + 1, :] = jnp.zeros((1, elements), F32)
-            target[RIM + REST * c : RIM + REST * (c + 1), :] = source[c, FN:NODES, :]
-        target[RIM + 3 * REST :, :] = jnp.zeros((ROWS - RIM - 3 * REST, elements), F32)
-    f[FN : FN + 1, :] = inv
 
     spread = spread_ref[...]
     mass = dot(dot(spread, mi_ref[...]), spread, ((1,), (1,))) * same_ref[...]
@@ -203,11 +315,11 @@
                 th[3 * RIM + at : 3 * RIM + at + 16, here] = low
                 th[6 * RIM + at : 6 * RIM + at + 16, here] = high
 
-    def rim(advance, width=2 * LANES):
+    def rim(keep, last=False, width=2 * LANES):
         for at in range(0, elements, width):
             lanes = pl.ds(at, width)
             jump = p[:, lanes] - f[0:RIM, lanes]
-            pull = jnp.concatenate(
+            pulled = jnp.concatenate(
                 traction(
                     [jump[16 * c : 16 * (c + 1), :] for c in range(3)],
                     [zc[c : c + 1, lanes] for c in range(3)],
@@ -216,99 +328,43 @@
                 ),
                 axis=0,
             )
-            high, low = halves(pull)
+            high, low = halves(pulled)
             change = jnp.dot(
                 zmat[...], jnp.concatenate([high, low, high], axis=0), preferred_element_type=F32
             )
+            if last:
+                f[:, lanes] = change
+                continue
             v[:, lanes] = v[:, lanes] + change
             f[:, lanes] = fp[:, lanes] + DT * change
-            if advance:
-                p[:, lanes] = tp[:, lanes] - (DT * ratio[0:1, lanes]) * change[0:RIM, :]
-
-    def cross_copy(turn, b, t):
-        return pltpu.make_async_remote_copy(
-            src_ref=xs.at[turn, b * SUBS + t],
-            dst_ref=xr.at[turn, (GROUPS - 2 - b) * SUBS + s],
-            send_sem=xs_sem.at[turn],
-            recv_sem=xr_sem.at[turn],
-            device_id=(lax.rem(g + 1 + b, GROUPS), t),
-            device_id_type=MESH,
-        )
-
-    def side_copy(turn, side):
-        return pltpu.make_async_remote_copy(
-            src_ref=ns.at[turn, side],
-            dst_ref=nr.at[turn, 1 - side],
-            send_sem=ns_sem.at[turn, side],
-            recv_sem=nr_sem.at[turn, 1 - side],
-            device_id=(g, down if side else up),
-            device_id_type=MESH,
-        )
-
-    blank = jnp.zeros((LANES - 2 * RIM, LANES), F32)
-
-    def send(turn):
-        for block in range((GROUPS - 1) * SUBS * SLOT // LANES):
-            lanes = pl.ds((2 + block) * LANES, LANES)
-            tile = jnp.concatenate([f[0:RIM, lanes], fp[0:RIM, lanes], blank], axis=0)
-            per = LANES // SLOT
-            xs[turn, block * per : (block + 1) * per, :, :] = tile.T.reshape(per, SLOT, LANES)
-        for side in range(2):
-            lanes = pl.ds(side * LANES, LANES)
-            ns[turn, side, 0:RIM, :] = f[0:RIM, lanes]
-            ns[turn, side, RIM:, :] = fp[0:RIM, lanes]
-
-        def go(k, carry):
-            t = lax.rem(s + k, SUBS)
-            for b in range(GROUPS - 1):
-                cross_copy(turn, b, t).start()
-            return carry
-
-        lax.fori_loop(0, SUBS, go, 0)
-        for side in range(2):
-            side_copy(turn, side).start()
-
-    def receive(turn):
-        for side in range(2):
-            side_copy(turn, 1 - side).wait_recv()
-            lanes = pl.ds(side * LANES, LANES)
-            p[:, lanes] = nr[turn, side, 0:RIM, :]
-            tp[:, lanes] = nr[turn, side, RIM:, :]
-        pltpu.make_async_copy(xr.at[turn], xr.at[turn], xr_sem.at[turn]).wait()
-        for block in range((GROUPS - 1) * SUBS * SLOT // LANES):
-            lanes = pl.ds((2 + block) * LANES, LANES)
-            per = LANES // SLOT
-            tile = xr[turn, block * per : (block + 1) * per, :, :].reshape(LANES, LANES).T
-            p[:, lanes] = tile[0:RIM, :]
-            tp[:, lanes] = tile[RIM : 2 * RIM, :]
-
-    local()
-    pl.semaphore_wait(barrier, (GROUPS - 1) * SUBS + 2)
+            if keep:
+                ch[:, lanes] = change[0:RIM, :]
 
     def pair(turn, carry):
-        @pl.when(turn > 0)
-        def _():
-            local()
-
-        send(turn)
-        receive(turn)
-        ratio[...] = p[FN : FN + 1, :] * jac_ref[...].reshape(1, elements)
+        local()
+        pack(2 * turn + 1, fp)
+        send(2 * turn + 1)
+        receive(2 * turn, p)
+        ratio[...] = p[FN : FN + 1, :] * (jac_ref[...].reshape(1, elements) * -DT)
         rim(True)
         local()
+        receive(2 * turn + 1, p)
+        for at in range(0, elements, 2 * LANES):
+            lanes = pl.ds(at, 2 * LANES)
+            p[:, lanes] = p[:, lanes] + ratio[0:1, lanes] * ch[:, lanes]
         rim(False)
+        pack(2 * turn + 2, f)
+        send(2 * turn + 2)
         return carry
 
     lax.fori_loop(0, ROUNDS - 1, pair, 0)
-    send(ROUNDS - 1)
     local()
-    receive(ROUNDS - 1)
-    rim(False)
-
-    for source, target in ((f, od_ref), (v, ov_ref)):
-        for c in range(3):
-            target[c, 0:FN, :] = source[16 * c : 16 * c + FN, :]
-            target[c, FN:NODES, :] = source[RIM + REST * c : RIM + REST * (c + 1), :]
-    for turn in range(ROUNDS):
+    empty(v, ovp)
+    empty(fp, ofp)
+    receive(2 * ROUNDS - 2, p)
+    rim(False, True)
+    empty(f, oc)
+    for turn in range(MESSAGES):
         pltpu.make_async_copy(xs.at[turn], xs.at[turn], xs_sem.at[turn]).wait()
         for side in range(2):
             side_copy(turn, side).wait_send()
@@ -316,17 +372,17 @@
 
 def shards(*args):
     elements = args[0].shape[2]
-    args = args[:4] + (args[4].T,) + args[5:]
-    consts = tuple(jnp.asarray(t) for t in tables())
     shape = jax.ShapeDtypeStruct(args[0].shape, F32)
+    args = args[:4] + (args[4].T,) + args[5:] + tuple(jnp.asarray(t) for t in tables())
     slots = (GROUPS - 1) * SUBS
     vmem = pl.BlockSpec(memory_space=pltpu.VMEM)
-    return pl.pallas_call(
+    speed, place, change = pl.pallas_call(
         kernel,
-        out_shape=(shape, shape),
-        in_specs=[vmem] * (len(args) + len(consts)),
-        out_specs=(vmem, vmem),
-        scratch_shapes=[
+        out_shape=(shape, shape, shape),
+        in_specs=[pl.BlockSpec(memory_space=pl.ANY)] * len(args),
+        out_specs=(vmem, vmem, vmem),
+        scratch_shapes=[pltpu.VMEM(a.shape, a.dtype) for a in args]
+        + [
             pltpu.VMEM((ROWS, elements), F32),
             pltpu.VMEM((ROWS, elements), F32),
             pltpu.VMEM((ROWS, elements), F32),
@@ -344,17 +400,19 @@
             pltpu.VMEM((3, 5, elements), F32),
             pltpu.VMEM((3, 2, elements), jnp.int32),
             pltpu.VMEM((5, elements), F32),
-            pltpu.VMEM((ROUNDS, slots, SLOT, LANES), F32),
-            pltpu.VMEM((ROUNDS, slots, SLOT, LANES), F32),
-            pltpu.VMEM((ROUNDS, 2, 2 * RIM, LANES), F32),
-            pltpu.VMEM((ROUNDS, 2, 2 * RIM, LANES), F32),
-            pltpu.SemaphoreType.DMA((ROUNDS,)),
-            pltpu.SemaphoreType.DMA((ROUNDS,)),
-            pltpu.SemaphoreType.DMA((ROUNDS, 2)),
-            pltpu.SemaphoreType.DMA((ROUNDS, 2)),
+            pltpu.VMEM((MESSAGES, slots, LINES, LANES), F32),
+            pltpu.VMEM((MESSAGES, slots, LINES, LANES), F32),
+            pltpu.VMEM((MESSAGES, 2, RIM, LANES), F32),
+            pltpu.VMEM((MESSAGES, 2, RIM, LANES), F32),
+            pltpu.SemaphoreType.DMA((len(args),)),
+            pltpu.SemaphoreType.DMA((MESSAGES,)),
+            pltpu.SemaphoreType.DMA((MESSAGES,)),
+            pltpu.SemaphoreType.DMA((MESSAGES, 2)),
+            pltpu.SemaphoreType.DMA((MESSAGES, 2)),
         ],
         compiler_params=pltpu.CompilerParams(collective_id=0, has_side_effects=True),
-    )(*args, *consts)
+    )(*args)
+    return place + DT * change, speed + change
 
 
 def solution(mesh):

time: 49.8 us -> 44.5 us (0.89)
  Pallas kernels: 46.3 us -> 41.3 us
  local copies, waits for them, and re-layouts: 2.69 us -> 0 us
  other arithmetic: 0 us -> 2.41 us
    pallas_call x1, Pallas kernels: 46.3 us -> 41.3 us  [shards(): pl.pallas_call(kernel, out_shape=(shape, shape, shape), in_specs=[pl.Bloc...]
    unnamed x4 -> x0, local copies, waits for them, and re-layouts: 2.69 us -> none
    add x0 -> x1, other arithmetic: none -> 2.41 us  [shards(): return (place + DT * change, speed + change)]
where the time goes in v3:
time: 44.5 us; the launch traced here: 44.3 us
  Pallas kernels  41.3 us (93%)
  other arithmetic  2.41 us (5%)
  between operations  0.64 us (1%)
    pallas_call x1, Pallas kernels, shards(): pl.pallas_call(kernel, out_shape=(shape, shape, shape), in_specs=[pl.Bloc...  41.3 us
    add x1, other arithmetic, shards(): return (place + DT * change, speed + change)  2.41 us

profile of v3, /device:TPU:1, one launch (start us, length us, event | category | flops | bytes accessed | tf_op | source)
XLA Modules:
  0.0 44.3 jit_solution(6403412304299960568)
XLA Ops:
  0.6 41.3 %shard_map.194 = (f32[3,35,1024]{2,1,0:T(8,128)}, f32[3,35,1024]{2,1,0:T(8,128)}, f32[3,35,1024]{2,1,0:T(8,128)}) custom-call(f32[3,35,1024]{2,1,0:T(8,128)} %refs_0_.1, f32[3,35,1024]{2,1,0:T(8,128)} %refs_1_.1, f32[6,1024]{1,0:T(8,128)} %refs_2_.1, f32[1024]{0:T(1024)} %refs_3_.1, f32[105,630]{1,0:T(8,128)} %bitcast.1, f32[15,15]{1,0:T(8,128)} %refs_5_.1, ...), custom_call_target="tpu_custom_call" | custom-call | tf_op jit(solution)/shard_map/pallas_call | solution.py:379
  41.9 2.4 %fusion = (f32[3,35,1024]{2,1,0:T(8,128)}, f32[3,35,1024]{2,1,0:T(8,128)}) fusion(f32[3,35,1024]{2,1,0:T(8,128)} %get-tuple-element.7, f32[3,35,1024]{2,1,0:T(8,128)} %get-tuple-element.6, f32[3,35,1024]{2,1,0:T(8,128)} %get-tuple-element.5), kind=kLoop, calls=%fused_computation.1 | loop fusion | flops 322560 | bytes 2150400 | tf_op jit(solution)/shard_map/add | solution.py:415

commit v4 on v3

--- a/solution.py
+++ b/solution.py
@@ -1,5 +1,3 @@
-import functools
-
 import jax
 import jax.numpy as jnp
 import numpy as np
@@ -9,7 +7,6 @@
 from jax.sharding import PartitionSpec as P
 
 MESH = pl.DeviceIdType.MESH
-HIGHEST = lax.Precision.HIGHEST
 F32 = jnp.float32
 BF16 = jnp.bfloat16
 
@@ -58,11 +55,16 @@
     same = ((comp[:, None] == comp[None, :]) & (comp[:, None] >= 0)).astype(np.float32)
     block = np.arange(4 * RIM) // 16
     same_face = (block[:, None] == block[None, :]).astype(np.float32)
-    return spread, perm, select, place, same, same_face
+    return spread, perm.T.copy(), select, place, same, same_face
+
+
+def one(a, b, dims=((1,), (0,))):
+    return lax.dot_general(a, b, (dims, ((), ())), preferred_element_type=F32)
 
 
 def dot(a, b, dims=((1,), (0,))):
-    return lax.dot_general(a, b, (dims, ((), ())), precision=HIGHEST, preferred_element_type=F32)
+    a, b = halves(a), halves(b)
+    return one(a[0], b[0], dims) + (one(a[0], b[1], dims) + one(a[1], b[0], dims))
 
 
 def halves(x):
@@ -107,7 +109,7 @@
             )
         return carry
 
-    lax.fori_loop(0, SUBS, greet, 0)
+    lax.fori_loop(0, SUBS, greet, 0, unroll=4)
     for t in (up, down):
         pl.semaphore_signal(barrier, inc=1, device_id=(g, t), device_id_type=MESH)
     first = (NAMES.index("displacement"), NAMES.index("jacobian"))
@@ -180,7 +182,7 @@
                 cross_copy(turn, b, t).start()
             return carry
 
-        lax.fori_loop(0, SUBS, go, 0)
+        lax.fori_loop(0, SUBS, go, 0, unroll=4)
         for side in range(2):
             side_copy(turn, side).start()
 
@@ -211,8 +213,6 @@
             target[c, FN:NODES, :] = source[RIM + REST * c : RIM + REST * (c + 1), :]
 
     pack(0, f)
-    pl.semaphore_wait(barrier, (GROUPS - 1) * SUBS + 2)
-    send(0)
 
     for k in range(count):
         if k not in first:
@@ -245,6 +245,18 @@
 
     spread = spread_ref[...]
     mass = dot(dot(spread, mi_ref[...]), spread, ((1,), (1,))) * same_ref[...]
+    flip = perm_ref[...].astype(BF16)
+    strain = halves(s_ref[...])
+    turned = one(flip, strain[0]) + one(flip, strain[1])
+    left = [one(x, flip).astype(BF16) for x in halves(mass)]
+    scaled = one(left[0], strain[0]) + (one(left[0], strain[1]) + one(left[1], strain[0]))
+    for m in range(PIECES):
+        columns = slice(m * 3 * NODES, (m + 1) * 3 * NODES)
+        high, low = halves(dot(scaled[:, columns], turned[:, columns], ((1,), (1,))))
+        rows = slice(m * ROWS, (m + 1) * ROWS)
+        amat[rows, 0:ROWS] = high
+        amat[rows, ROWS : 2 * ROWS] = high
+        amat[rows, 2 * ROWS : 3 * ROWS] = low
     place = place_ref[...]
     face = dot(dot(place, fm_ref[...], ((0,), (0,))), place) * face_ref[...]
     lift = dot(mass, dot(select_ref[...], face, ((0,), (0,))))
@@ -255,14 +267,6 @@
     lmat[:, 0 : 3 * RIM] = high[:, RIM:]
     lmat[:, 3 * RIM : 6 * RIM] = high[:, RIM:]
     lmat[:, 6 * RIM : 9 * RIM] = low[:, RIM:]
-    turned = dot(perm_ref[...], s_ref[...], ((0,), (0,)))
-    for m in range(PIECES):
-        piece = turned[:, m * 3 * NODES : (m + 1) * 3 * NODES]
-        high, low = halves(dot(mass, dot(piece, piece, ((1,), (1,)))))
-        rows = slice(m * ROWS, (m + 1) * ROWS)
-        amat[rows, 0:ROWS] = high
-        amat[rows, ROWS : 2 * ROWS] = high
-        amat[rows, 2 * ROWS : 3 * ROWS] = low
     chosen = select_ref[RIM:, :].astype(BF16)
     smat[:, 0:ROWS] = chosen
     smat[:, ROWS : 2 * ROWS] = chosen
@@ -357,6 +361,9 @@
         send(2 * turn + 2)
         return carry
 
+    pl.semaphore_wait(barrier, (GROUPS - 1) * SUBS + 2)
+    send(0)
+
     lax.fori_loop(0, ROUNDS - 1, pair, 0)
     local()
     empty(v, ovp)
@@ -378,7 +385,7 @@
     vmem = pl.BlockSpec(memory_space=pltpu.VMEM)
     speed, place, change = pl.pallas_call(
         kernel,
-        out_shape=(shape, shape, shape),
+        out_shape=(pltpu.VMEM(shape.shape, F32),) * 3,
         in_specs=[pl.BlockSpec(memory_space=pl.ANY)] * len(args),
         out_specs=(vmem, vmem, vmem),
         scratch_shapes=[pltpu.VMEM(a.shape, a.dtype) for a in args]

time: 44.5 us -> 38.4 us (0.86)
  Pallas kernels: 41.3 us -> 36.6 us
  other arithmetic: 2.41 us -> 1.04 us
    pallas_call x1, Pallas kernels: 41.3 us -> 36.6 us  [shards(): pl.pallas_call(kernel, out_shape=(pltpu.VMEM(shape.shape, F32),) * 3, in_...]
    add x1, other arithmetic: 2.41 us -> 1.04 us  [shards(): return (place + DT * change, speed + change)]
where the time goes in v4:
time: 38.4 us; the launch traced here: 38.3 us
  Pallas kernels  36.6 us (95%)
  other arithmetic  1.04 us (3%)
  between operations  0.64 us (2%)
    pallas_call x1, Pallas kernels, shards(): pl.pallas_call(kernel, out_shape=(pltpu.VMEM(shape.shape, F32),) * 3, in_...  36.6 us
    add x1, other arithmetic, shards(): return (place + DT * change, speed + change)  1.04 us

profile of v4, /device:TPU:1, one launch (start us, length us, event | category | flops | bytes accessed | tf_op | source)
XLA Modules:
  0.0 38.3 jit_solution(18417644537930671437)
XLA Ops:
  0.6 36.6 %shard_map.194 = (f32[3,35,1024]{2,1,0:T(8,128)S(1)}, f32[3,35,1024]{2,1,0:T(8,128)S(1)}, f32[3,35,1024]{2,1,0:T(8,128)S(1)}) custom-call(f32[3,35,1024]{2,1,0:T(8,128)} %refs_0_.1, f32[3,35,1024]{2,1,0:T(8,128)} %refs_1_.1, f32[6,1024]{1,0:T(8,128)} %refs_2_.1, f32[1024]{0:T(1024)} %refs_3_.1, f32[105,630]{1,0:T(8,128)} %bitcast.1, f32[15,15]{1,0:T(8,128)} %refs_5_.1, ...), custom_call_target="tpu_custom_call" | custom-call | tf_op jit(solution)/shard_map/pallas_call | solution.py:386
  37.2 1.0 %fusion = (f32[3,35,1024]{2,1,0:T(8,128)}, f32[3,35,1024]{2,1,0:T(8,128)}) fusion(f32[3,35,1024]{2,1,0:T(8,128)S(1)} %get-tuple-element.7, f32[3,35,1024]{2,1,0:T(8,128)S(1)} %get-tuple-element.6, f32[3,35,1024]{2,1,0:T(8,128)S(1)} %get-tuple-element.5), kind=kLoop, calls=%fused_computation.1 | loop fusion | flops 322560 | bytes 2150400 | tf_op jit(solution)/shard_map/add | solution.py:422

commit v5 on v4

--- a/solution.py
+++ b/solution.py
@@ -29,6 +29,10 @@
     "side_links", "side_geometry", "cross_links", "cross_geometry",
     "spread", "perm", "select", "place", "same", "face",
 )
+
+
+def reach(k):
+    return -sum(min(d, 4 - d) for d in (k // 8, k // 2 % 4))
 
 
 def row_of(c, n):
@@ -176,13 +180,10 @@
             ns[turn, side, :, :] = source[0:RIM, pl.ds(side * LANES, LANES)]
 
     def send(turn):
-        def go(k, carry):
+        for k in sorted(range(SUBS), key=reach):
             t = lax.rem(s + k, SUBS)
-            for b in range(GROUPS - 1):
+            for b in (1, 0, 2):
                 cross_copy(turn, b, t).start()
-            return carry
-
-        lax.fori_loop(0, SUBS, go, 0, unroll=4)
         for side in range(2):
             side_copy(turn, side).start()
 
@@ -277,11 +278,12 @@
             high, low = halves(f[:, lanes])
             fh[0:ROWS, lanes] = high
             fh[ROWS : 2 * ROWS, lanes] = low
-            fh[2 * ROWS :, lanes] = high
             tr[:, lanes] = jnp.dot(smat[...], fh[0 : 2 * ROWS, lanes], preferred_element_type=F32)
         for at in range(0, elements, width):
             lanes = pl.ds(at, width)
-            product = jnp.dot(amat[...], fh[:, lanes], preferred_element_type=F32)
+            product = jnp.dot(
+                amat[...], jnp.concatenate([fh[:, lanes], fh[0:ROWS, lanes]], axis=0), preferred_element_type=F32
+            )
             change = wj[0:1, lanes] * product[0:ROWS, :]
             for m in range(1, PIECES):
                 change = change + wj[m : m + 1, lanes] * product[m * ROWS : (m + 1) * ROWS, :]
@@ -290,7 +292,9 @@
                 pull(block)
         for at in range(0, elements, width):
             lanes = pl.ds(at, width)
-            speed = v[:, lanes] + jnp.dot(lmat[...], th[:, lanes], preferred_element_type=F32)
+            speed = v[:, lanes] + jnp.dot(
+                lmat[...], jnp.concatenate([th[:, lanes], th[0 : 3 * RIM, lanes]], axis=0), preferred_element_type=F32
+            )
             v[:, lanes] = speed
             fp[:, lanes] = f[:, lanes] + DT * speed
 
@@ -317,7 +321,6 @@
                 at = q * RIM + 16 * c
                 th[at : at + 16, here] = high
                 th[3 * RIM + at : 3 * RIM + at + 16, here] = low
-                th[6 * RIM + at : 6 * RIM + at + 16, here] = high
 
     def rim(keep, last=False, width=2 * LANES):
         for at in range(0, elements, width):
@@ -399,9 +402,9 @@
             pltpu.VMEM((3 * RIM, 2 * ROWS), BF16),
             pltpu.VMEM((ROWS, 9 * RIM), BF16),
             pltpu.VMEM((ROWS, 3 * RIM), BF16),
-            pltpu.VMEM((3 * ROWS, elements), BF16),
+            pltpu.VMEM((2 * ROWS, elements), BF16),
             pltpu.VMEM((3 * RIM, elements), F32),
-            pltpu.VMEM((9 * RIM, elements), BF16),
+            pltpu.VMEM((6 * RIM, elements), BF16),
             pltpu.VMEM((PIECES, elements), F32),
             pltpu.VMEM((1, elements), F32),
             pltpu.VMEM((3, 5, elements), F32),

time: 38.4 us -> 37.3 us (0.971)
  Pallas kernels: 36.6 us -> 35.4 us
    pallas_call x1, Pallas kernels: 36.6 us -> 35.4 us  [shards(): pl.pallas_call(kernel, out_shape=(pltpu.VMEM(shape.shape, F32),) * 3, in_...]
where the time goes in v5:
time: 37.3 us; the launch traced here: 37.1 us
  Pallas kernels  35.4 us (95%)
  other arithmetic  1.04 us (3%)
  between operations  0.64 us (2%)
    pallas_call x1, Pallas kernels, shards(): pl.pallas_call(kernel, out_shape=(pltpu.VMEM(shape.shape, F32),) * 3, in_...  35.4 us
    add x1, other arithmetic, shards(): return (place + DT * change, speed + change)  1.04 us

profile of v5, /device:TPU:1, one launch (start us, length us, event | category | flops | bytes accessed | tf_op | source)
XLA Modules:
  0.0 37.1 jit_solution(14341251144450447045)
XLA Ops:
  0.6 35.4 %shard_map.194 = (f32[3,35,1024]{2,1,0:T(8,128)S(1)}, f32[3,35,1024]{2,1,0:T(8,128)S(1)}, f32[3,35,1024]{2,1,0:T(8,128)S(1)}) custom-call(f32[3,35,1024]{2,1,0:T(8,128)} %refs_0_.1, f32[3,35,1024]{2,1,0:T(8,128)} %refs_1_.1, f32[6,1024]{1,0:T(8,128)} %refs_2_.1, f32[1024]{0:T(1024)} %refs_3_.1, f32[105,630]{1,0:T(8,128)} %bitcast.1, f32[15,15]{1,0:T(8,128)} %refs_5_.1, ...), custom_call_target="tpu_custom_call" | custom-call | tf_op jit(solution)/shard_map/pallas_call | solution.py:389
  36.1 1.0 %fusion = (f32[3,35,1024]{2,1,0:T(8,128)}, f32[3,35,1024]{2,1,0:T(8,128)}) fusion(f32[3,35,1024]{2,1,0:T(8,128)S(1)} %get-tuple-element.7, f32[3,35,1024]{2,1,0:T(8,128)S(1)} %get-tuple-element.6, f32[3,35,1024]{2,1,0:T(8,128)S(1)} %get-tuple-element.5), kind=kLoop, calls=%fused_computation.1 | loop fusion | flops 322560 | bytes 2150400 | tf_op jit(solution)/shard_map/add | solution.py:425

commit v6 on v5

--- a/solution.py
+++ b/solution.py
@@ -106,14 +106,11 @@
     down = lax.rem(s + SUBS - 1, SUBS)
     barrier = pltpu.get_barrier_semaphore()
 
-    def greet(t, carry):
-        for b in range(GROUPS - 1):
+    for k in sorted(range(SUBS), key=reach):
+        for b in (1, 0, 2):
             pl.semaphore_signal(
-                barrier, inc=1, device_id=(lax.rem(g + 1 + b, GROUPS), t), device_id_type=MESH
-            )
-        return carry
-
-    lax.fori_loop(0, SUBS, greet, 0, unroll=4)
+                barrier, inc=1, device_id=(lax.rem(g + 1 + b, GROUPS), lax.rem(s + k, SUBS)), device_id_type=MESH
+            )
     for t in (up, down):
         pl.semaphore_signal(barrier, inc=1, device_id=(g, t), device_id_type=MESH)
     first = (NAMES.index("displacement"), NAMES.index("jacobian"))

time: 37.3 us -> 37.2 us (level)
  no operation moved by 1% of the time
where the time goes in v6:
time: 37.2 us; the launch traced here: 37.1 us
  Pallas kernels  35.4 us (95%)
  other arithmetic  1.04 us (3%)
  between operations  0.64 us (2%)
    pallas_call x1, Pallas kernels, shards(): pl.pallas_call(kernel, out_shape=(pltpu.VMEM(shape.shape, F32),) * 3, in_...  35.4 us
    add x1, other arithmetic, shards(): return (place + DT * change, speed + change)  1.04 us

profile of v6, /device:TPU:1, one launch (start us, length us, event | category | flops | bytes accessed | tf_op | source)
XLA Modules:
  0.0 37.1 jit_solution(11949218127795345473)
XLA Ops:
  0.6 35.4 %shard_map.194 = (f32[3,35,1024]{2,1,0:T(8,128)S(1)}, f32[3,35,1024]{2,1,0:T(8,128)S(1)}, f32[3,35,1024]{2,1,0:T(8,128)S(1)}) custom-call(f32[3,35,1024]{2,1,0:T(8,128)} %refs_0_.1, f32[3,35,1024]{2,1,0:T(8,128)} %refs_1_.1, f32[6,1024]{1,0:T(8,128)} %refs_2_.1, f32[1024]{0:T(1024)} %refs_3_.1, f32[105,630]{1,0:T(8,128)} %bitcast.1, f32[15,15]{1,0:T(8,128)} %refs_5_.1, ...), custom_call_target="tpu_custom_call" | custom-call | tf_op jit(solution)/shard_map/pallas_call | solution.py:386
  36.0 1.0 %fusion = (f32[3,35,1024]{2,1,0:T(8,128)}, f32[3,35,1024]{2,1,0:T(8,128)}) fusion(f32[3,35,1024]{2,1,0:T(8,128)S(1)} %get-tuple-element.7, f32[3,35,1024]{2,1,0:T(8,128)S(1)} %get-tuple-element.6, f32[3,35,1024]{2,1,0:T(8,128)S(1)} %get-tuple-element.5), kind=kLoop, calls=%fused_computation.1 | loop fusion | flops 322560 | bytes 2150400 | tf_op jit(solution)/shard_map/add | solution.py:422
